TPU v7x, 32 devices: a whole 2x2x4 slice. The times are simulated.
32 devices in a mesh: cluster: 8 (over z, y), sub: 4 (over x, core).
Axes of the slice: x: 2, y: 2, z: 4, core: 2. Of those that a mesh axis runs over, the one named last changes fastest.
Arguments:
- right_side: float32 [4, 8, 16, 384], P('sub', 'cluster'), may hold values from -12 to 12
- schur: float32 [4, 8, 768, 768], P('sub', 'cluster'), as said below
- rigid_modes: float32 [4, 8, 6, 768], P('sub', 'cluster'), may hold values from -0.21875 to 0.21875
- mode_count: int32 [4, 8], P('sub', 'cluster'), may hold values from 3 to 6
- face_order: int32 [4, 8, 384], P('sub', 'cluster'), may hold values from 0 to 383, each once within a row
- dual_scale: float32 [4, 8, 384], P('sub', 'cluster'), may hold values from 0.5 to 2
- rigid_loads: float32 [4, 8, 6, 16], P('sub', 'cluster'), may hold values from -6 to 6
- coarse_inverse: float32 [192, 192], P(('cluster', 'sub')), as said below
Outputs:
- multipliers: float32 [4, 8, 16, 384], P('sub', 'cluster')
- residual: float32 [4, 8, 16, 384], P('sub', 'cluster')
Inputs may be any that keep to these rules, and one draw needn't show every extreme that they name: rigid-body modes m with m >= mode_count are unused. `face_order`: each subdomain's entries form a permutation of the face unknowns; those of the first subdomain of a chain are unused. `schur`: each subdomain's matrix is symmetric. `coarse_inverse`: symmetric.
All inputs are finite; a program needn't handle non-finite values.
Results may differ from a plain program's by a relative error of at most 0.0003.
Values sent between devices are 32-bit elements; how exact they have to be, the bound alone decides.
No kernel may reach another device: no remote copies, remote signals or barrier semaphores. Data moves between devices by JAX's collectives and lax.ppermute only.
A program may use at most 64 MiB of HBM per device.

v0:
```python
import jax
import jax.numpy as jnp
from jax import lax
from jax.sharding import PartitionSpec as P

ITERS = 2
highest = lax.Precision.HIGHEST


def from_behind(block, axis, distance):
    devices = range(lax.axis_size(axis))
    route = [(i - distance, i) for i in devices if i - distance in devices]
    return lax.ppermute(block, axis, route)


def permute_faces(field, index):

    def single_face(values, order):
        return jnp.take(values, order, axis=1)

    return jax.vmap(jax.vmap(single_face))(field, index)


def lift_faces(dual_field, face_order):
    incoming = from_behind(dual_field, "cluster", 1)
    earlier = jnp.concatenate([incoming, dual_field[:, :-1]], axis=1)
    left_face = -permute_faces(earlier, face_order)
    return jnp.concatenate([left_face, dual_field], axis=3)


def push_faces(values, inverse):
    half_size = values.shape[3] // 2
    left_face = values[..., :half_size]
    right_face = values[..., half_size:]
    returned = -permute_faces(left_face, inverse)
    outgoing = from_behind(returned, "cluster", -1)
    following = jnp.concatenate([returned[:, 1:], outgoing], axis=1)
    return right_face + following


def apply_dual(dual_field, schur, face_order, inverse):
    lifted = lift_faces(dual_field, face_order)
    dual_image = jnp.einsum("sjci,sjik->sjck", lifted, schur, precision=highest)
    return push_faces(dual_image, inverse)


def basis_transpose(dual_field, basis, face_order):
    return jnp.einsum(
        "sjmi,sjci->sjmc", basis, lift_faces(dual_field, face_order), precision=highest
    )


def basis_expand(coefficients, basis, inverse):
    return push_faces(
        jnp.einsum("sjmi,sjmc->sjci", basis, coefficients, precision=highest), inverse
    )


def coarse_plain(coefficients, coarse_rows):
    flattened = coefficients.reshape(-1, coefficients.shape[3])
    solved = lax.psum_scatter(
        jnp.dot(coarse_rows.T, flattened, precision=highest),
        ("cluster", "sub"),
        scatter_dimension=0,
        tiled=True,
    )
    return solved.reshape(coefficients.shape)


def project(dual_field, basis, face_order, inverse, coarse_rows):
    coefficients = basis_transpose(dual_field, basis, face_order)
    return dual_field - basis_expand(coarse_plain(coefficients, coarse_rows), basis, inverse)


def gram_product(first_field, second_field):
    return jnp.einsum("sjcm,sjdm->cd", first_field, second_field, precision=highest)


def solve_small(matrix, right_hand):
    factor = jnp.linalg.cholesky(matrix)
    halfway = lax.linalg.triangular_solve(factor, right_hand, left_side=True, lower=True)
    return lax.linalg.triangular_solve(
        factor, halfway, left_side=True, lower=True, transpose_a=True
    )


def step_quantities(dual_image, direction, residual, basis, face_order, inverse, coarse_rows):
    curvature_part = gram_product(direction, dual_image)
    descent_part = gram_product(direction, residual)
    coefficients = basis_transpose(dual_image, basis, face_order)
    curvature, descent = lax.psum((curvature_part, descent_part), ("cluster", "sub"))
    solved = coarse_plain(coefficients, coarse_rows)
    projected_image = dual_image - basis_expand(solved, basis, inverse)
    return (curvature, descent, projected_image)


def shards(
    right_side, schur, rigid_modes, mode_count, face_order, dual_scale, rigid_loads, coarse_inverse
):
    inverse = jnp.argsort(face_order, axis=-1)
    active = (jnp.arange(rigid_modes.shape[2])[None, None, :] < mode_count[:, :, None]).astype(
        jnp.float32
    )
    basis = rigid_modes * active[..., None]
    masked_loads = rigid_loads * active[..., None]
    scaling = dual_scale[:, :, None, :]
    multipliers = basis_expand(coarse_plain(masked_loads, coarse_inverse), basis, inverse)
    residual = project(
        right_side - apply_dual(multipliers, schur, face_order, inverse),
        basis,
        face_order,
        inverse,
        coarse_inverse,
    )
    search = project(scaling * residual, basis, face_order, inverse, coarse_inverse)
    direction = search
    for iteration in range(ITERS):
        dual_image = apply_dual(direction, schur, face_order, inverse)
        curvature, descent, projected_image = step_quantities(
            dual_image, direction, residual, basis, face_order, inverse, coarse_inverse
        )
        step_size = solve_small(curvature, descent)
        multipliers = multipliers + jnp.einsum(
            "sjcm,cd->sjdm", direction, step_size, precision=highest
        )
        residual = residual - jnp.einsum(
            "sjcm,cd->sjdm", projected_image, step_size, precision=highest
        )
        if iteration + 1 < ITERS:
            search = project(scaling * residual, basis, face_order, inverse, coarse_inverse)
            update = lax.psum(gram_product(dual_image, search), ("cluster", "sub"))
            correction = -solve_small(curvature, update)
            direction = search + jnp.einsum(
                "sjcm,cd->sjdm", direction, correction, precision=highest
            )
    return (multipliers, residual)


def solution(mesh):
    in_specs = (
        P("sub", "cluster", None, None),
        P("sub", "cluster", None, None),
        P("sub", "cluster", None, None),
        P("sub", "cluster"),
        P("sub", "cluster", None),
        P("sub", "cluster", None),
        P("sub", "cluster", None, None),
        P(("cluster", "sub"), None),
    )
    out_specs = (P("sub", "cluster", None, None), P("sub", "cluster", None, None))
    return jax.shard_map(shards, mesh=mesh, in_specs=in_specs, out_specs=out_specs, check_vma=False)
```

profile of v0, /device:TPU:6, one launch (start us, length us, event | category | flops | bytes accessed | tf_op | source)
XLA Modules:
  0.0 495.1 jit_solution(11295149442735976061)
XLA Ops:
  9.6 40.4 %all-reduce = f32[192,16]{0,1:T(8,128)S(1)} all-reduce(f32[192,16]{0,1:T(8,128)S(1)} %convolution_bitcast_fusion.16), channel_id=2, replica_groups=mesh['cluster'=8,'sub'=4] {'cluster','sub'}, use_global_device_ids=true, to_apply=%region_0.0.clone | all-reduce | flops 3072 | bytes 24576
  52.7 3.8 gather_fusion
  56.6 3.4 collective-permute-start
  60.7 2.5 collective-permute-done
  63.3 3.4 collective-permute-start.1
  69.1 3.8 gather_fusion.1
  74.5 3.8 gather_fusion.2
  80.4 4.7 collective-permute-done.2
  85.1 3.4 collective-permute-start.3
  90.9 3.8 gather_fusion.3
  95.3 41.6 %all-reduce.1 = f32[192,16]{0,1:T(8,128)S(1)} all-reduce(f32[192,16]{0,1:T(8,128)S(1)} %convolution_bitcast_fusion.15), channel_id=3, replica_groups=mesh['cluster'=8,'sub'=4] {'cluster','sub'}, use_global_device_ids=true, to_apply=%region_2.4.clone | all-reduce | flops 3072 | bytes 24576
  137.2 3.8 gather_fusion.4
  141.2 2.5 collective-permute-start.4
  143.7 4.1 collective-permute-done.4
  149.7 3.8 collective-permute-done.5
  153.7 3.8 gather_fusion.5
  158.0 39.5 %all-reduce.2 = f32[192,16]{0,1:T(8,128)S(1)} all-reduce(f32[192,16]{0,1:T(8,128)S(1)} %convolution_bitcast_fusion.14), channel_id=4, replica_groups=mesh['cluster'=8,'sub'=4] {'cluster','sub'}, use_global_device_ids=true, to_apply=%region_3.5.clone | all-reduce | flops 3072 | bytes 24576
  197.9 3.8 gather_fusion.6
  201.9 3.0 collective-permute-start.6
  204.9 3.6 collective-permute-done.6
  208.5 3.2 collective-permute-start.7
  211.7 2.5 collective-permute-done.7
  214.4 3.8 gather_fusion.7
  219.7 3.8 gather_fusion.8
  225.7 4.6 collective-permute-done.8
  230.4 2.9 collective-permute-start.9
  233.4 2.7 collective-permute-done.9
  236.2 3.8 gather_fusion.9
  240.5 40.7 %all-reduce.7 = (f32[16,16]{1,0:T(8,128)S(1)}, f32[16,16]{0,1:T(8,128)S(1)}, f32[192,16]{0,1:T(8,128)S(1)}) all-reduce(f32[16,16]{1,0:T(8,128)S(1)} %fusion.99, f32[16,16]{0,1:T(8,128)S(1)} %fusion.102, f32[192,16]{0,1:T(8,128)S(1)} %convolution_bitcast_fusion.13), channel_id=1, replica_groups=mesh['cluster'=8,'sub'=4] {'cluster','sub'}, use_global_device_ids=true, to_apply=%region_7.10 | all-reduce | flops 3584 | bytes 28672 | tf_op jit(solution)/shard_map/psum | solution.py:91
  285.8 3.8 gather_fusion.10
  292.5 3.8 collective-permute-done.10
  298.8 3.5 collective-permute-done.11
  302.4 3.8 gather_fusion.11
  306.8 39.6 %all-reduce.4 = f32[192,16]{0,1:T(8,128)S(1)} all-reduce(f32[192,16]{0,1:T(8,128)S(1)} %convolution_bitcast_fusion.12), channel_id=6, replica_groups=mesh['cluster'=8,'sub'=4] {'cluster','sub'}, use_global_device_ids=true, to_apply=%region_9.0.clone | all-reduce | flops 3072 | bytes 24576
  346.8 3.8 gather_fusion.12
  350.7 2.9 collective-permute-start.12
  353.7 3.7 collective-permute-done.12
  357.5 40.5 %psum.37 = f32[16,16]{1,0:T(8,128)S(1)} all-reduce(f32[16,16]{1,0:T(8,128)S(1)} %fusion.97), channel_id=1, replica_groups=mesh['cluster'=8,'sub'=4] {'cluster','sub'}, use_global_device_ids=true, to_apply=%region_10.0 | all-reduce | flops 256 | bytes 2048 | tf_op jit(solution)/shard_map/psum | solution.py:131
  398.6 2.9 collective-permute-start.13
  401.5 2.8 collective-permute-done.13
  404.5 3.8 gather_fusion.13
  409.8 3.8 gather_fusion.14
  415.8 4.5 collective-permute-done.14
  420.4 3.1 collective-permute-start.15
  426.2 3.8 gather_fusion.15
  430.6 40.7 %all-reduce.6 = (f32[16,16]{1,0:T(8,128)S(1)}, f32[16,16]{0,1:T(8,128)S(1)}, f32[192,16]{0,1:T(8,128)S(1)}) all-reduce(f32[16,16]{1,0:T(8,128)S(1)} %fusion.90, f32[16,16]{0,1:T(8,128)S(1)} %fusion.92, f32[192,16]{0,1:T(8,128)S(1)} %convolution_bitcast_fusion.11), channel_id=1, replica_groups=mesh['cluster'=8,'sub'=4] {'cluster','sub'}, use_global_device_ids=true, to_apply=%region_12.0 | all-reduce | flops 3584 | bytes 28672 | tf_op jit(solution)/shard_map/psum | solution.py:91
  476.4 3.8 gather_fusion.16
  483.2 3.7 collective-permute-done.16
  (148 shorter events, 49.4 us)
Async XLA Ops:
  7.2 65.9 %copy-start = (f32[1,1,768,768]{3,2,1,0:T(8,128)S(1)}, f32[1,1,768,768]{3,2,1,0:T(8,128)}, u32[]{:S(2)}) copy-start(f32[1,1,768,768]{3,2,1,0:T(8,128)} %param.16) | copy-start | bytes 7077892
  7.2 44.1 %sort.19.cloned.1.call-start = ((), (), s32[]{:S(2)}) async-start(), calls=%async_computation | async-start | bytes 9248 | tf_op jit(solution)/shard_map/jit(argsort)/sort | solution.py:100
  56.5 28.5 %copy-start.2 = (f32[1,1,16,384]{3,2,1,0:T(8,128)S(1)}, f32[1,1,16,384]{3,2,1,0:T(8,128)}, u32[]{:S(2)}) copy-start(f32[1,1,16,384]{3,2,1,0:T(8,128)} %param.15) | copy-start | bytes 73732
  56.6 6.6 %collective-permute-start = (f32[1,1,16,384]{3,2,1,0:T(8,128)S(1)}, f32[1,1,16,384]{3,2,1,0:T(8,128)S(1)}, u32[]{:S(2)}, u32[]{:S(2)}) collective-permute-start(f32[1,1,16,384]{3,2,1,0:T(8,128)S(1)} %fusion.89), channel_id=1, source_target_pairs={{4,0},{8,4},{12,8},{16,12},{20,16},{24,20},{28,24},{5,1},{9,5},{13... | collective-permute-start | bytes 73736 | tf_op jit(solution)/shard_map/ppermute | solution.py:13
  63.3 5.7 %collective-permute-start.1 = (f32[1,1,16,384]{3,2,1,0:T(8,128)S(1)}, f32[1,1,16,384]{3,2,1,0:T(8,128)S(1)}, u32[]{:S(2)}, u32[]{:S(2)}) collective-permute-start(f32[1,1,16,384]{3,2,1,0:T(8,128)S(1)} %slice_add_fusion.8), channel_id=1, source_target_pairs={{0,4},{4,8},{8,12},{12,16},{16,20},{20,24},{24,28},{1,5},{5,9},{9,... | collective-permute-start | bytes 73736 | tf_op jit(solution)/shard_map/ppermute | solution.py:13
  73.0 22.1 %copy-start.1 = (f32[6,192]{1,0:T(8,128)S(1)}, f32[6,192]{1,0:T(8,128)}, u32[]{:S(2)}) copy-start(f32[6,192]{1,0:T(8,128)} %param.22) | copy-start | bytes 13828
  73.1 70.6 %copy-start.3 = (f32[1,1,384]{2,1,0:T(1,128)S(1)}, f32[1,1,384]{2,1,0:T(1,128)}, u32[]{:S(2)}) copy-start(f32[1,1,384]{2,1,0:T(1,128)} %param.20) | copy-start | bytes 4612
  78.4 6.6 %collective-permute-start.2 = (f32[1,1,16,384]{3,2,1,0:T(8,128)S(1)}, f32[1,1,16,384]{3,2,1,0:T(8,128)S(1)}, u32[]{:S(2)}, u32[]{:S(2)}) collective-permute-start(f32[1,1,16,384]{3,2,1,0:T(8,128)S(1)} %fusion.87), channel_id=1, source_target_pairs={{4,0},{8,4},{12,8},{16,12},{20,16},{24,20},{28,24},{5,1},{9,5},{13... | collective-permute-start | bytes 73736 | tf_op jit(solution)/shard_map/ppermute | solution.py:13
  85.1 5.7 %collective-permute-start.3 = (f32[1,1,16,384]{3,2,1,0:T(8,128)S(1)}, f32[1,1,16,384]{3,2,1,0:T(8,128)S(1)}, u32[]{:S(2)}, u32[]{:S(2)}) collective-permute-start(f32[1,1,16,384]{3,2,1,0:T(8,128)S(1)} %fusion.50), channel_id=1, source_target_pairs={{0,4},{4,8},{8,12},{12,16},{16,20},{20,24},{24,28},{1,5},{5,9},{9,... | collective-permute-start | bytes 73736 | tf_op jit(solution)/shard_map/ppermute | solution.py:13
  141.2 6.6 %collective-permute-start.4 = (f32[1,1,16,384]{3,2,1,0:T(8,128)S(1)}, f32[1,1,16,384]{3,2,1,0:T(8,128)S(1)}, u32[]{:S(2)}, u32[]{:S(2)}) collective-permute-start(f32[1,1,16,384]{3,2,1,0:T(8,128)S(1)} %fusion.85), channel_id=1, source_target_pairs={{4,0},{8,4},{12,8},{16,12},{20,16},{24,20},{28,24},{5,1},{9,5},{13... | collective-permute-start | bytes 73736 | tf_op jit(solution)/shard_map/ppermute | solution.py:13
  147.8 5.7 %collective-permute-start.5 = (f32[1,1,16,384]{3,2,1,0:T(8,128)S(1)}, f32[1,1,16,384]{3,2,1,0:T(8,128)S(1)}, u32[]{:S(2)}, u32[]{:S(2)}) collective-permute-start(f32[1,1,16,384]{3,2,1,0:T(8,128)S(1)} %get-tuple-element.14), channel_id=1, source_target_pairs={{0,4},{4,8},{8,12},{12,16},{16,20},{20,24},{24,28},{1,5},{5,9},{9,... | collective-permute-start | bytes 73736 | tf_op jit(solution)/shard_map/ppermute | solution.py:13
  201.9 6.6 %collective-permute-start.6 = (f32[1,1,16,384]{3,2,1,0:T(8,128)S(1)}, f32[1,1,16,384]{3,2,1,0:T(8,128)S(1)}, u32[]{:S(2)}, u32[]{:S(2)}) collective-permute-start(f32[1,1,16,384]{3,2,1,0:T(8,128)S(1)} %fusion.83), channel_id=1, source_target_pairs={{4,0},{8,4},{12,8},{16,12},{20,16},{24,20},{28,24},{5,1},{9,5},{13... | collective-permute-start | bytes 73736 | tf_op jit(solution)/shard_map/ppermute | solution.py:13
  208.5 5.7 %collective-permute-start.7 = (f32[1,1,16,384]{3,2,1,0:T(8,128)S(1)}, f32[1,1,16,384]{3,2,1,0:T(8,128)S(1)}, u32[]{:S(2)}, u32[]{:S(2)}) collective-permute-start(f32[1,1,16,384]{3,2,1,0:T(8,128)S(1)} %fusion.48), channel_id=1, source_target_pairs={{0,4},{4,8},{8,12},{12,16},{16,20},{20,24},{24,28},{1,5},{5,9},{9,... | collective-permute-start | bytes 73736 | tf_op jit(solution)/shard_map/ppermute | solution.py:13
  223.6 6.7 %collective-permute-start.8 = (f32[1,1,16,384]{3,2,1,0:T(8,128)S(1)}, f32[1,1,16,384]{3,2,1,0:T(8,128)S(1)}, u32[]{:S(2)}, u32[]{:S(2)}) collective-permute-start(f32[1,1,16,384]{3,2,1,0:T(8,128)S(1)} %fusion.81), channel_id=1, source_target_pairs={{4,0},{8,4},{12,8},{16,12},{20,16},{24,20},{28,24},{5,1},{9,5},{13... | collective-permute-start | bytes 73736 | tf_op jit(solution)/shard_map/ppermute | solution.py:13
  230.4 5.7 %collective-permute-start.9 = (f32[1,1,16,384]{3,2,1,0:T(8,128)S(1)}, f32[1,1,16,384]{3,2,1,0:T(8,128)S(1)}, u32[]{:S(2)}, u32[]{:S(2)}) collective-permute-start(f32[1,1,16,384]{3,2,1,0:T(8,128)S(1)} %slice_add_fusion.4), channel_id=1, source_target_pairs={{0,4},{4,8},{8,12},{12,16},{16,20},{20,24},{24,28},{1,5},{5,9},{9,... | collective-permute-start | bytes 73736 | tf_op jit(solution)/shard_map/ppermute | solution.py:13
  289.7 6.6 %collective-permute-start.10 = (f32[1,1,16,384]{3,2,1,0:T(8,128)S(1)}, f32[1,1,16,384]{3,2,1,0:T(8,128)S(1)}, u32[]{:S(2)}, u32[]{:S(2)}) collective-permute-start(f32[1,1,16,384]{3,2,1,0:T(8,128)S(1)} %fusion.79), channel_id=1, source_target_pairs={{4,0},{8,4},{12,8},{16,12},{20,16},{24,20},{28,24},{5,1},{9,5},{13... | collective-permute-start | bytes 73736 | tf_op jit(solution)/shard_map/ppermute | solution.py:13
  296.6 5.7 %collective-permute-start.11 = (f32[1,1,16,384]{3,2,1,0:T(8,128)S(1)}, f32[1,1,16,384]{3,2,1,0:T(8,128)S(1)}, u32[]{:S(2)}, u32[]{:S(2)}) collective-permute-start(f32[1,1,16,384]{3,2,1,0:T(8,128)S(1)} %get-tuple-element.18), channel_id=1, source_target_pairs={{0,4},{4,8},{8,12},{12,16},{16,20},{20,24},{24,28},{1,5},{5,9},{9,... | collective-permute-start | bytes 73736 | tf_op jit(solution)/shard_map/ppermute | solution.py:13
  350.7 6.6 %collective-permute-start.12 = (f32[1,1,16,384]{3,2,1,0:T(8,128)S(1)}, f32[1,1,16,384]{3,2,1,0:T(8,128)S(1)}, u32[]{:S(2)}, u32[]{:S(2)}) collective-permute-start(f32[1,1,16,384]{3,2,1,0:T(8,128)S(1)} %fusion.77), channel_id=1, source_target_pairs={{4,0},{8,4},{12,8},{16,12},{20,16},{24,20},{28,24},{5,1},{9,5},{13... | collective-permute-start | bytes 73736 | tf_op jit(solution)/shard_map/ppermute | solution.py:13
  398.6 5.7 %collective-permute-start.13 = (f32[1,1,16,384]{3,2,1,0:T(8,128)S(1)}, f32[1,1,16,384]{3,2,1,0:T(8,128)S(1)}, u32[]{:S(2)}, u32[]{:S(2)}) collective-permute-start(f32[1,1,16,384]{3,2,1,0:T(8,128)S(1)} %fusion.18), channel_id=1, source_target_pairs={{0,4},{4,8},{8,12},{12,16},{16,20},{20,24},{24,28},{1,5},{5,9},{9,... | collective-permute-start | bytes 73736 | tf_op jit(solution)/shard_map/ppermute | solution.py:13
  413.7 6.6 %collective-permute-start.14 = (f32[1,1,16,384]{3,2,1,0:T(8,128)S(1)}, f32[1,1,16,384]{3,2,1,0:T(8,128)S(1)}, u32[]{:S(2)}, u32[]{:S(2)}) collective-permute-start(f32[1,1,16,384]{3,2,1,0:T(8,128)S(1)} %fusion.75), channel_id=1, source_target_pairs={{4,0},{8,4},{12,8},{16,12},{20,16},{24,20},{28,24},{5,1},{9,5},{13... | collective-permute-start | bytes 73736 | tf_op jit(solution)/shard_map/ppermute | solution.py:13
  420.4 5.7 %collective-permute-start.15 = (f32[1,1,16,384]{3,2,1,0:T(8,128)S(1)}, f32[1,1,16,384]{3,2,1,0:T(8,128)S(1)}, u32[]{:S(2)}, u32[]{:S(2)}) collective-permute-start(f32[1,1,16,384]{3,2,1,0:T(8,128)S(1)} %slice_add_fusion.1), channel_id=1, source_target_pairs={{0,4},{4,8},{8,12},{12,16},{16,20},{20,24},{24,28},{1,5},{5,9},{9,... | collective-permute-start | bytes 73736 | tf_op jit(solution)/shard_map/ppermute | solution.py:13
  480.3 6.6 %collective-permute-start.16 = (f32[1,1,16,384]{3,2,1,0:T(8,128)S(1)}, f32[1,1,16,384]{3,2,1,0:T(8,128)S(1)}, u32[]{:S(2)}, u32[]{:S(2)}) collective-permute-start(f32[1,1,16,384]{3,2,1,0:T(8,128)S(1)} %fusion.73), channel_id=1, source_target_pairs={{4,0},{8,4},{12,8},{16,12},{20,16},{24,20},{28,24},{5,1},{9,5},{13... | collective-permute-start | bytes 73736 | tf_op jit(solution)/shard_map/ppermute | solution.py:13
Sparse Core Ops, SparseCore 0:
  10.9 2.7 sort.21.cloned.1.call-done
  (1 shorter events, 0.0 us)
where the time goes:
time: 504 us; the launch traced here: 495 us
  blocking collectives  283 us (56%)
  local copies, waits for them, and re-layouts  69.8 us (14%)
  waiting for transfers between devices  57.6 us (11%)
  starting transfers between devices  45.2 us (9%)
  between operations  15.9 us (3%)
  matrix products  12.3 us (2%)
  other arithmetic  11.2 us (2%)
    unnamed x4, blocking collectives  161 us
    psum x2, blocking collectives, step_quantities(): lax.psum((curvature_part, descent_part), ('cluster', 'sub'))  81.4 us
    gather x34, local copies, waits for them, and re-layouts, single_face(): return jnp.take(values, order, axis=1)  66.8 us
    ppermute x17, waiting for transfers between devices, from_behind(): return lax.ppermute(block, axis, route)  57.6 us
    ppermute x17, starting transfers between devices, from_behind(): return lax.ppermute(block, axis, route)  45.2 us
    psum x1, blocking collectives, shards(): update = lax.psum(gram_product(dual_image, search), ('cluster', 'sub'))  40.5 us
  transfers between devices with their start and end apart: 17, of which 17 were waited for; matrix products, arithmetic and copies ran while one was open for 1% of the time, Pallas kernels for 0%

commit v1 on v0

--- a/solution.py
+++ b/solution.py
@@ -2,6 +2,7 @@
 import jax.numpy as jnp
 from jax import lax
 from jax.sharding import PartitionSpec as P
+from jax.lax import psum
 
 ITERS = 2
 highest = lax.Precision.HIGHEST
@@ -88,7 +89,8 @@
     curvature_part = gram_product(direction, dual_image)
     descent_part = gram_product(direction, residual)
     coefficients = basis_transpose(dual_image, basis, face_order)
-    curvature, descent = lax.psum((curvature_part, descent_part), ("cluster", "sub"))
+    _load_arrays = lambda mat: psum(psum(mat, "sub"), "cluster")
+    curvature, descent = _load_arrays((curvature_part, descent_part))
     solved = coarse_plain(coefficients, coarse_rows)
     projected_image = dual_image - basis_expand(solved, basis, inverse)
     return (curvature, descent, projected_image)

time: 504 us -> 585 us (1.16)
  blocking collectives: 283 us -> 367 us
  waiting for transfers between devices: 57.6 us -> 50.1 us
    unnamed x4 -> x6, blocking collectives: 161 us -> 245 us
    ppermute x17, waiting for transfers between devices: 57.6 us -> 50.1 us  [from_behind(): return lax.ppermute(block, axis, route)]
    psum x2 -> x4, blocking collectives: 81.4 us -> 82.2 us  [step_quantities(): _load_arrays = lambda mat: psum(psum(mat, 'sub'), 'cluster')]
  transfers between devices with their start and end apart: 17 -> 17, of which waited for: 17 -> 15; matrix products, arithmetic and copies ran while one was open for 1% -> 2% of each run, Pallas kernels for 0% -> 0%
where the time goes in v1:
time: 585 us; the launch traced here: 575 us
  blocking collectives  367 us (63%)
  local copies, waits for them, and re-layouts  69.8 us (12%)
  waiting for transfers between devices  50.1 us (9%)
  starting transfers between devices  48.5 us (8%)
  between operations  15.9 us (3%)
  matrix products  12.3 us (2%)
  other arithmetic  11.2 us (2%)
    unnamed x6, blocking collectives  245 us
    psum x4, blocking collectives, step_quantities(): _load_arrays = lambda mat: psum(psum(mat, 'sub'), 'cluster')  82.2 us
    gather x34, local copies, waits for them, and re-layouts, single_face(): return jnp.take(values, order, axis=1)  66.8 us
    ppermute x17, waiting for transfers between devices, from_behind(): return lax.ppermute(block, axis, route)  50.1 us
    ppermute x17, starting transfers between devices, from_behind(): return lax.ppermute(block, axis, route)  48.5 us
    psum x1, blocking collectives, shards(): update = lax.psum(gram_product(dual_image, search), ('cluster', 'sub'))  39.7 us
  transfers between devices with their start and end apart: 17, of which 15 were waited for; matrix products, arithmetic and copies ran while one was open for 2% of the time, Pallas kernels for 0%

profile of v1, /device:TPU:6, one launch (start us, length us, event | category | flops | bytes accessed | tf_op | source)
XLA Modules:
  0.0 574.9 jit_solution(12891280061495667047)
XLA Ops:
  9.6 40.4 %all-reduce = f32[192,16]{0,1:T(8,128)S(1)} all-reduce(f32[192,16]{0,1:T(8,128)S(1)} %convolution_bitcast_fusion.16), channel_id=2, replica_groups=mesh['cluster'=8,'sub'=4] {'cluster','sub'}, use_global_device_ids=true, to_apply=%region_0.0.clone | all-reduce | flops 3072 | bytes 24576
  52.7 3.8 gather_fusion
  56.6 3.4 collective-permute-start
  63.3 3.4 collective-permute-start.1
  69.1 3.8 gather_fusion.1
  74.5 3.8 gather_fusion.2
  80.4 4.7 collective-permute-done.2
  85.1 3.4 collective-permute-start.3
  90.9 3.8 gather_fusion.3
  95.3 41.6 %all-reduce.1 = f32[192,16]{0,1:T(8,128)S(1)} all-reduce(f32[192,16]{0,1:T(8,128)S(1)} %convolution_bitcast_fusion.15), channel_id=3, replica_groups=mesh['cluster'=8,'sub'=4] {'cluster','sub'}, use_global_device_ids=true, to_apply=%region_2.4.clone | all-reduce | flops 3072 | bytes 24576
  137.2 3.8 gather_fusion.4
  143.7 4.1 collective-permute-done.4
  149.7 3.8 collective-permute-done.5
  153.7 3.8 gather_fusion.5
  158.0 39.5 %all-reduce.2 = f32[192,16]{0,1:T(8,128)S(1)} all-reduce(f32[192,16]{0,1:T(8,128)S(1)} %convolution_bitcast_fusion.14), channel_id=4, replica_groups=mesh['cluster'=8,'sub'=4] {'cluster','sub'}, use_global_device_ids=true, to_apply=%region_3.5.clone | all-reduce | flops 3072 | bytes 24576
  197.9 3.8 gather_fusion.6
  201.9 3.0 collective-permute-start.6
  204.9 3.6 collective-permute-done.6
  208.5 3.2 collective-permute-start.7
  211.7 2.5 collective-permute-done.7
  214.3 3.8 gather_fusion.7
  219.7 3.8 gather_fusion.8
  225.7 4.6 collective-permute-done.8
  230.4 3.0 collective-permute-start.9
  233.4 10.1 %all-reduce.9 = (f32[16,16]{1,0:T(8,128)S(1)}, f32[16,16]{0,1:T(8,128)S(1)}) all-reduce(f32[16,16]{1,0:T(8,128)S(1)} %fusion.99, f32[16,16]{0,1:T(8,128)S(1)} %fusion.102), channel_id=1, replica_groups=mesh['cluster'=8,'sub'=4] {'sub'}, use_global_device_ids=true, to_apply=%region_8.11 | all-reduce | flops 512 | bytes 4096 | tf_op jit(solution)/shard_map/psum | solution.py:92
  243.6 31.1 %all-reduce.7 = (f32[16,16]{1,0:T(8,128)S(1)}, f32[16,16]{0,1:T(8,128)S(1)}) all-reduce(f32[16,16]{1,0:T(8,128)S(1)} %get-tuple-element.14, f32[16,16]{0,1:T(8,128)S(1)} %get-tuple-element.15), channel_id=1, replica_groups=mesh['cluster'=8,'sub'=4] {'cluster'}, use_global_device_ids=true, to_apply=%region_9.12 | all-reduce | flops 512 | bytes 4096 | tf_op jit(solution)/shard_map/psum | solution.py:92
  279.1 3.8 gather_fusion.9
  283.5 40.9 %all-reduce.3 = f32[192,16]{0,1:T(8,128)S(1)} all-reduce(f32[192,16]{0,1:T(8,128)S(1)} %convolution_bitcast_fusion.13), channel_id=5, replica_groups=mesh['cluster'=8,'sub'=4] {'cluster','sub'}, use_global_device_ids=true, to_apply=%region_10.0.clone | all-reduce | flops 3072 | bytes 24576
  324.8 3.8 gather_fusion.10
  331.1 4.3 collective-permute-done.10
  335.6 3.7 collective-permute-start.11
  341.5 3.8 gather_fusion.11
  345.8 41.1 %all-reduce.4 = f32[192,16]{0,1:T(8,128)S(1)} all-reduce(f32[192,16]{0,1:T(8,128)S(1)} %convolution_bitcast_fusion.12), channel_id=6, replica_groups=mesh['cluster'=8,'sub'=4] {'cluster','sub'}, use_global_device_ids=true, to_apply=%region_11.0.clone | all-reduce | flops 3072 | bytes 24576
  387.4 3.8 gather_fusion.12
  391.3 3.7 collective-permute-start.12
  395.0 3.0 collective-permute-done.12
  398.1 39.7 %psum.67 = f32[16,16]{1,0:T(8,128)S(1)} all-reduce(f32[16,16]{1,0:T(8,128)S(1)} %fusion.97), channel_id=1, replica_groups=mesh['cluster'=8,'sub'=4] {'cluster','sub'}, use_global_device_ids=true, to_apply=%region_12.0 | all-reduce | flops 256 | bytes 2048 | tf_op jit(solution)/shard_map/psum | solution.py:133
  438.4 3.7 collective-permute-start.13
  444.2 3.8 gather_fusion.13
  449.6 3.8 gather_fusion.14
  455.6 4.5 collective-permute-done.14
  460.3 3.7 collective-permute-start.15
  464.0 10.1 %all-reduce.8 = (f32[16,16]{1,0:T(8,128)S(1)}, f32[16,16]{0,1:T(8,128)S(1)}) all-reduce(f32[16,16]{1,0:T(8,128)S(1)} %fusion.90, f32[16,16]{0,1:T(8,128)S(1)} %fusion.92), channel_id=1, replica_groups=mesh['cluster'=8,'sub'=4] {'sub'}, use_global_device_ids=true, to_apply=%region_15.0 | all-reduce | flops 512 | bytes 4096 | tf_op jit(solution)/shard_map/psum | solution.py:92
  474.2 30.8 %all-reduce.6 = (f32[16,16]{1,0:T(8,128)S(1)}, f32[16,16]{0,1:T(8,128)S(1)}) all-reduce(f32[16,16]{1,0:T(8,128)S(1)} %get-tuple-element.12, f32[16,16]{0,1:T(8,128)S(1)} %get-tuple-element.13), channel_id=1, replica_groups=mesh['cluster'=8,'sub'=4] {'cluster'}, use_global_device_ids=true, to_apply=%region_16.0 | all-reduce | flops 512 | bytes 4096 | tf_op jit(solution)/shard_map/psum | solution.py:92
  509.8 3.8 gather_fusion.15
  514.1 41.6 %all-reduce.5 = f32[192,16]{0,1:T(8,128)S(1)} all-reduce(f32[192,16]{0,1:T(8,128)S(1)} %convolution_bitcast_fusion.11), channel_id=7, replica_groups=mesh['cluster'=8,'sub'=4] {'cluster','sub'}, use_global_device_ids=true, to_apply=%region_17.22.clone | all-reduce | flops 3072 | bytes 24576
  556.2 3.8 gather_fusion.16
  562.9 3.8 collective-permute-done.16
  (152 shorter events, 53.3 us)
Async XLA Ops:
  7.2 65.9 %copy-start = (f32[1,1,768,768]{3,2,1,0:T(8,128)S(1)}, f32[1,1,768,768]{3,2,1,0:T(8,128)}, u32[]{:S(2)}) copy-start(f32[1,1,768,768]{3,2,1,0:T(8,128)} %param.16) | copy-start | bytes 7077892
  7.2 44.1 %sort.19.cloned.1.call-start = ((), (), s32[]{:S(2)}) async-start(), calls=%async_computation | async-start | bytes 9248 | tf_op jit(solution)/shard_map/jit(argsort)/sort | solution.py:102
  56.5 28.5 %copy-start.2 = (f32[1,1,16,384]{3,2,1,0:T(8,128)S(1)}, f32[1,1,16,384]{3,2,1,0:T(8,128)}, u32[]{:S(2)}) copy-start(f32[1,1,16,384]{3,2,1,0:T(8,128)} %param.15) | copy-start | bytes 73732
  56.6 6.6 %collective-permute-start = (f32[1,1,16,384]{3,2,1,0:T(8,128)S(1)}, f32[1,1,16,384]{3,2,1,0:T(8,128)S(1)}, u32[]{:S(2)}, u32[]{:S(2)}) collective-permute-start(f32[1,1,16,384]{3,2,1,0:T(8,128)S(1)} %fusion.89), channel_id=1, source_target_pairs={{4,0},{8,4},{12,8},{16,12},{20,16},{24,20},{28,24},{5,1},{9,5},{13... | collective-permute-start | bytes 73736 | tf_op jit(solution)/shard_map/ppermute | solution.py:14
  63.3 5.7 collective-permute-start.1
  73.0 22.1 %copy-start.1 = (f32[6,192]{1,0:T(8,128)S(1)}, f32[6,192]{1,0:T(8,128)}, u32[]{:S(2)}) copy-start(f32[6,192]{1,0:T(8,128)} %param.22) | copy-start | bytes 13828
  73.1 70.6 %copy-start.3 = (f32[1,1,384]{2,1,0:T(1,128)S(1)}, f32[1,1,384]{2,1,0:T(1,128)}, u32[]{:S(2)}) copy-start(f32[1,1,384]{2,1,0:T(1,128)} %param.20) | copy-start | bytes 4612
  78.4 6.6 %collective-permute-start.2 = (f32[1,1,16,384]{3,2,1,0:T(8,128)S(1)}, f32[1,1,16,384]{3,2,1,0:T(8,128)S(1)}, u32[]{:S(2)}, u32[]{:S(2)}) collective-permute-start(f32[1,1,16,384]{3,2,1,0:T(8,128)S(1)} %fusion.87), channel_id=1, source_target_pairs={{4,0},{8,4},{12,8},{16,12},{20,16},{24,20},{28,24},{5,1},{9,5},{13... | collective-permute-start | bytes 73736 | tf_op jit(solution)/shard_map/ppermute | solution.py:14
  85.1 5.7 collective-permute-start.3
  141.2 6.6 %collective-permute-start.4 = (f32[1,1,16,384]{3,2,1,0:T(8,128)S(1)}, f32[1,1,16,384]{3,2,1,0:T(8,128)S(1)}, u32[]{:S(2)}, u32[]{:S(2)}) collective-permute-start(f32[1,1,16,384]{3,2,1,0:T(8,128)S(1)} %fusion.85), channel_id=1, source_target_pairs={{4,0},{8,4},{12,8},{16,12},{20,16},{24,20},{28,24},{5,1},{9,5},{13... | collective-permute-start | bytes 73736 | tf_op jit(solution)/shard_map/ppermute | solution.py:14
  147.8 5.7 collective-permute-start.5
  201.9 6.6 %collective-permute-start.6 = (f32[1,1,16,384]{3,2,1,0:T(8,128)S(1)}, f32[1,1,16,384]{3,2,1,0:T(8,128)S(1)}, u32[]{:S(2)}, u32[]{:S(2)}) collective-permute-start(f32[1,1,16,384]{3,2,1,0:T(8,128)S(1)} %fusion.83), channel_id=1, source_target_pairs={{4,0},{8,4},{12,8},{16,12},{20,16},{24,20},{28,24},{5,1},{9,5},{13... | collective-permute-start | bytes 73736 | tf_op jit(solution)/shard_map/ppermute | solution.py:14
  208.5 5.7 collective-permute-start.7
  223.6 6.6 %collective-permute-start.8 = (f32[1,1,16,384]{3,2,1,0:T(8,128)S(1)}, f32[1,1,16,384]{3,2,1,0:T(8,128)S(1)}, u32[]{:S(2)}, u32[]{:S(2)}) collective-permute-start(f32[1,1,16,384]{3,2,1,0:T(8,128)S(1)} %fusion.81), channel_id=1, source_target_pairs={{4,0},{8,4},{12,8},{16,12},{20,16},{24,20},{28,24},{5,1},{9,5},{13... | collective-permute-start | bytes 73736 | tf_op jit(solution)/shard_map/ppermute | solution.py:14
  230.4 48.6 %collective-permute-start.9 = (f32[1,1,16,384]{3,2,1,0:T(8,128)S(1)}, f32[1,1,16,384]{3,2,1,0:T(8,128)S(1)}, u32[]{:S(2)}, u32[]{:S(2)}) collective-permute-start(f32[1,1,16,384]{3,2,1,0:T(8,128)S(1)} %slice_add_fusion.4), channel_id=1, source_target_pairs={{0,4},{4,8},{8,12},{12,16},{16,20},{20,24},{24,28},{1,5},{5,9},{9,... | collective-permute-start | bytes 73736 | tf_op jit(solution)/shard_map/ppermute | solution.py:14
  328.8 6.6 %collective-permute-start.10 = (f32[1,1,16,384]{3,2,1,0:T(8,128)S(1)}, f32[1,1,16,384]{3,2,1,0:T(8,128)S(1)}, u32[]{:S(2)}, u32[]{:S(2)}) collective-permute-start(f32[1,1,16,384]{3,2,1,0:T(8,128)S(1)} %fusion.79), channel_id=1, source_target_pairs={{4,0},{8,4},{12,8},{16,12},{20,16},{24,20},{28,24},{5,1},{9,5},{13... | collective-permute-start | bytes 73736 | tf_op jit(solution)/shard_map/ppermute | solution.py:14
  335.6 5.7 collective-permute-start.11
  391.3 6.6 %collective-permute-start.12 = (f32[1,1,16,384]{3,2,1,0:T(8,128)S(1)}, f32[1,1,16,384]{3,2,1,0:T(8,128)S(1)}, u32[]{:S(2)}, u32[]{:S(2)}) collective-permute-start(f32[1,1,16,384]{3,2,1,0:T(8,128)S(1)} %fusion.77), channel_id=1, source_target_pairs={{4,0},{8,4},{12,8},{16,12},{20,16},{24,20},{28,24},{5,1},{9,5},{13... | collective-permute-start | bytes 73736 | tf_op jit(solution)/shard_map/ppermute | solution.py:14
  438.4 5.7 collective-permute-start.13
  453.5 6.6 %collective-permute-start.14 = (f32[1,1,16,384]{3,2,1,0:T(8,128)S(1)}, f32[1,1,16,384]{3,2,1,0:T(8,128)S(1)}, u32[]{:S(2)}, u32[]{:S(2)}) collective-permute-start(f32[1,1,16,384]{3,2,1,0:T(8,128)S(1)} %fusion.75), channel_id=1, source_target_pairs={{4,0},{8,4},{12,8},{16,12},{20,16},{24,20},{28,24},{5,1},{9,5},{13... | collective-permute-start | bytes 73736 | tf_op jit(solution)/shard_map/ppermute | solution.py:14
  460.3 49.3 %collective-permute-start.15 = (f32[1,1,16,384]{3,2,1,0:T(8,128)S(1)}, f32[1,1,16,384]{3,2,1,0:T(8,128)S(1)}, u32[]{:S(2)}, u32[]{:S(2)}) collective-permute-start(f32[1,1,16,384]{3,2,1,0:T(8,128)S(1)} %slice_add_fusion.1), channel_id=1, source_target_pairs={{0,4},{4,8},{8,12},{12,16},{16,20},{20,24},{24,28},{1,5},{5,9},{9,... | collective-permute-start | bytes 73736 | tf_op jit(solution)/shard_map/ppermute | solution.py:14
  560.1 6.6 %collective-permute-start.16 = (f32[1,1,16,384]{3,2,1,0:T(8,128)S(1)}, f32[1,1,16,384]{3,2,1,0:T(8,128)S(1)}, u32[]{:S(2)}, u32[]{:S(2)}) collective-permute-start(f32[1,1,16,384]{3,2,1,0:T(8,128)S(1)} %fusion.73), channel_id=1, source_target_pairs={{4,0},{8,4},{12,8},{16,12},{20,16},{24,20},{28,24},{5,1},{9,5},{13... | collective-permute-start | bytes 73736 | tf_op jit(solution)/shard_map/ppermute | solution.py:14
Sparse Core Ops, SparseCore 0:
  10.9 2.7 sort.21.cloned.1.call-done
  (1 shorter events, 0.0 us)
